TPU v7x, 128 devices: a whole 4x4x4 slice. The times are simulated.
128 devices in a mesh: blk: 8 (over y, z_lo), seg: 16 (over x, z_hi, core).
Axes of the slice: x: 4, y: 4, z: 4 (z_hi: 2, z_lo: 2; z = z_hi * 2 + z_lo), core: 2. Of those that a mesh axis runs over, the one named last changes fastest.
Arguments:
- spectra: bfloat16 [16, 2, 4096, 2048], P('seg', None, 'blk'), may hold values from -6 to 6
- window_count: int32 [16], P('seg'), may hold values from 1 to 2, as said below
- tile_owner: int32 [8, 80], P('blk'), may hold values from 0 to 15, as said below
- phases: float32 [2, 128, 256], replicated, may hold values from -3.140625 to 3.140625
Outputs:
- tile_power: float32 [8, 16, 8, 2, 256], P('blk', 'seg')
Inputs may be any that keep to these rules, and one draw needn't show every extreme that they name: `window_count`: the largest value, 2, occurs in every draw. `tile_owner`: in each row no segment index occurs more than 8 times, and some index occurs exactly 8 times.
All inputs are finite; a program needn't handle non-finite values.
Results may differ from a plain program's by a relative error of at most 0.004.
Values may be sent and summed in bfloat16 or wider, within the bound.
A program may use at most 128 MiB of HBM per device.

v0:
```python
import math

import jax
import jax.numpy as jnp
from jax import lax
from jax.sharding import PartitionSpec as P

TILE = 128
BANDS = 2
CAP = 8
FB = 512
QUAD = 4


def from_behind(array, axis, by):
    devices = lax.axis_size(axis)
    return lax.ppermute(array, axis, [(i, (i + by) % devices) for i in range(devices)])


def prepare(segment_data, counted):
    windows = segment_data.shape[0]
    channels = segment_data.shape[1]
    spectrum = segment_data.astype(jnp.float32).reshape(windows, channels, BANDS, 2, FB)
    scaling = lax.rsqrt(jnp.mean(spectrum * spectrum, axis=(2, 3, 4)) + 1e-05)
    live_mask = (jnp.arange(windows, dtype=jnp.int32) < counted).astype(jnp.float32)
    return (
        spectrum * scaling[:, :, None, None, None] * live_mask[:, None, None, None, None]
    ).astype(jnp.bfloat16)


def correlate(resident, visiting, weight):
    windows = resident.shape[0]
    flipped = jnp.stack([-visiting[:, :, :, 1], visiting[:, :, :, 0]], axis=3)
    both_parts = jnp.stack([visiting, flipped], axis=1)
    left_side = resident.reshape(windows, QUAD, TILE, BANDS, 2 * FB)
    right_side = both_parts.reshape(windows, 2, QUAD, TILE, BANDS, 2 * FB)
    product = jnp.einsum(
        "wqibk,wpsjbk->qsbipj", left_side, right_side, preferred_element_type=jnp.float32
    )
    return (product * weight).astype(jnp.bfloat16).reshape(QUAD * QUAD, BANDS, TILE, 2 * TILE)


def disperse(stacked, phases):
    velocity_count = phases.shape[2]
    norm_factor = 1.0 / math.sqrt(TILE)
    cosine = (jnp.cos(phases) * norm_factor).astype(jnp.bfloat16)
    sine_part = (jnp.sin(phases) * norm_factor).astype(jnp.bfloat16)
    upper = jnp.concatenate([cosine, sine_part], axis=2)
    lower = jnp.concatenate([-sine_part, cosine], axis=2)
    matrix = jnp.concatenate([upper, lower], axis=1)
    field = jnp.einsum("nbij,bjv->nbiv", stacked, matrix, preferred_element_type=jnp.float32)
    squared = field * field
    energy = squared[..., :velocity_count] + squared[..., velocity_count:]
    return jnp.mean(energy, axis=2)


def slot_table(owner_row, segments):
    count_tiles = owner_row.shape[0]
    order_ids = jnp.arange(count_tiles, dtype=jnp.int32)
    same_owner = owner_row[:, None] == owner_row[None, :]
    earlier = order_ids[None, :] < order_ids[:, None]
    rank_of = jnp.sum(jnp.where(same_owner & earlier, 1, 0), axis=1).astype(jnp.int32)
    slot_ids = owner_row * CAP + rank_of
    grid_ids = jnp.arange(segments * CAP, dtype=jnp.int32)
    matches = grid_ids[:, None] == slot_ids[None, :]
    tile_of_slot = jnp.sum(jnp.where(matches, order_ids[None, :], 0), axis=1)
    filled = jnp.any(matches, axis=1)
    return (tile_of_slot, filled)


def body(spectra, window_count, tile_owner, phases):
    blocks = lax.axis_size("blk")
    segments = lax.axis_size("seg")
    counted = window_count[0]
    whitened = prepare(spectra[0], counted)
    weight = 1.0 / (counted.astype(jnp.float32) * math.sqrt(FB * segments))
    pieces = [correlate(whitened, whitened, weight)]
    moving = whitened
    for shift_step in range(1, blocks // 2 + 1):
        moving = from_behind(moving, "blk", -1)
        pieces.append(correlate(whitened, moving, weight))
    all_tiles = jnp.concatenate(pieces, axis=0)
    tile_of_slot, filled = slot_table(tile_owner[0], segments)
    outgoing = jnp.take(all_tiles, tile_of_slot, axis=0)
    outgoing = jnp.where(filled[:, None, None, None], outgoing, jnp.zeros_like(outgoing))
    outgoing = outgoing.reshape(segments, CAP, BANDS, TILE, 2 * TILE)
    stacked = jnp.sum(
        lax.all_to_all(outgoing, "seg", split_axis=0, concat_axis=0, tiled=True),
        axis=0,
        dtype=jnp.float32,
    ).astype(jnp.bfloat16)
    response = disperse(stacked, phases)
    return response[None, None]


def solution(mesh):
    placed = (P("seg", None, "blk", None), P("seg"), P("blk", None), P())
    return jax.shard_map(
        body,
        mesh=mesh,
        in_specs=placed,
        out_specs=P("blk", "seg", None, None, None),
        check_vma=False,
    )
```

profile of v0, /device:TPU:1, one launch (start us, length us, event | category | flops | bytes accessed | tf_op | source)
XLA Modules:
  0.0 760.2 jit_solution(3550814971370002830)
XLA Ops:
  0.0 3.1 multiply_reduce_fusion
  3.1 11.5 %reshape.135 = f32[2,512,2,2,512]{4,3,2,1,0:T(2,128)} reshape(bf16[1,2,512,2048]{3,2,1,0:T(8,128)(2,1)} %param.4) | data formatting | bytes 12582912 | tf_op jit(solution)/shard_map/convert_element_type | solution.py:23
  15.3 7.3 fusion.14
  22.6 4.9 collective-permute-start
  27.5 11.5 %reshape.136 = f32[2,4,128,2,1024]{4,3,2,1,0:T(2,128)} reshape(bf16[1,2,512,2048]{3,2,1,0:T(8,128)(2,1)} %param.4) | data formatting | bytes 12582912 | tf_op jit(solution)/shard_map/convert_element_type | solution.py:23
  39.0 19.6 %copy.44 = f32[1,2,512,2048]{2,0,3,1:T(1,128)} copy(bf16[1,2,512,2048]{3,2,1,0:T(8,128)(2,1)} %param.4) | data formatting | bytes 12582912 | tf_op jit(solution)/shard_map/convert_element_type | solution.py:23
  58.7 10.9 %slice_negate_fusion.4 = (bf16[2,512,2,1,512]{4,3,1,2,0:T(2,128)(2,1)S(1)}, bf16[2,512,2,1,512]{4,3,1,2,0:T(2,128)(2,1)S(1)}) fusion(bf16[2,512,2,2,512]{4,3,1,2,0:T(2,128)(2,1)} %fusion.14), kind=kLoop, calls=%fused_computation.31 | loop fusion | flops 1048576 | bytes 8388608 | tf_op jit(solution)/shard_map/neg | solution.py:33
  69.5 47.5 %collective-permute-done = bf16[2,512,2,2,512]{4,3,1,2,0:T(2,128)(2,1)} collective-permute-done((bf16[2,512,2,2,512]{4,3,1,2,0:T(2,128)(2,1)}, bf16[2,512,2,2,512]{4,3,1,2,0:T(2,128)(2,1)}, u32[]{:S(2)}, u32[]{:S(2)}) %collective-permute-start) | collective-permute-done | bytes 4194336 | tf_op jit(solution)/shard_map/ppermute | solution.py:17
  117.0 4.8 collective-permute-start.1
  121.9 10.5 %pad_maximum_fusion = bf16[2,512,2,2,512]{4,3,1,2,0:T(2,128)(2,1)} fusion(bf16[2,512,2,1,512]{4,3,1,2,0:T(2,128)(2,1)S(1)} %get-tuple-element.16, bf16[2,512,2,1,512]{4,3,1,2,0:T(2,128)(2,1)S(1)} %get-tuple-element.15), kind=kLoop, calls=%fused_computation.32 | loop fusion | flops 8388608 | bytes 8388608 | tf_op jit(solution)/shard_map/stack | solution.py:33
  132.4 7.7 %stack.64 = bf16[2,1,4,128,2,1024]{5,3,2,4,0,1:T(8,128)(2,1)} reshape(bf16[2,512,2,2,512]{4,3,1,2,0:T(2,128)(2,1)} %pad_maximum_fusion) | data formatting | bytes 8388608 | tf_op jit(solution)/shard_map/stack | solution.py:34
  140.1 10.0 %copy.45 = f32[2,1,4,128,2,1024]{5,3,0,2,1,4:T(8,128)} copy(f32[2,1,4,128,2,1024]{3,2,1,5,4,0:T(4,128)} %bitcast.134) | data formatting | bytes 16777216 | tf_op jit(solution)/shard_map/convert_element_type | solution.py:23
  150.1 6.8 fusion.15
  156.9 0.8 multiply_convert_fusion
  157.8 1.3 copy-done.1
  159.1 1.6 copy-done.2
  160.6 4.7 fusion.30
  165.4 0.1 copy.49
  165.5 0.5 copy-done.4
  166.0 0.2 select_reduce_fusion.1
  166.6 1.5 constant_dynamic-update-slice_fusion.4
  168.1 42.4 %collective-permute-done.1 = bf16[2,512,2,2,512]{4,3,1,2,0:T(2,128)(2,1)} collective-permute-done((bf16[2,512,2,2,512]{4,3,1,2,0:T(2,128)(2,1)}, bf16[2,512,2,2,512]{4,3,1,2,0:T(2,128)(2,1)}, u32[]{:S(2)}, u32[]{:S(2)}) %collective-permute-start.1) | collective-permute-done | bytes 4194336 | tf_op jit(solution)/shard_map/ppermute | solution.py:17
  210.6 4.5 collective-permute-start.2
  215.0 11.0 %slice_negate_fusion.3 = (bf16[2,512,2,1,512]{4,3,1,2,0:T(2,128)(2,1)S(1)}, bf16[2,512,2,1,512]{4,3,1,2,0:T(2,128)(2,1)S(1)}) fusion(bf16[2,512,2,2,512]{4,3,1,2,0:T(2,128)(2,1)} %collective-permute-done), kind=kLoop, calls=%fused_computation.30 | loop fusion | flops 1048576 | bytes 8388608 | tf_op jit(solution)/shard_map/neg | solution.py:33
  226.0 10.5 %pad_maximum_fusion.1 = bf16[2,512,2,2,512]{4,3,1,2,0:T(2,128)(2,1)} fusion(bf16[2,512,2,1,512]{4,3,1,2,0:T(2,128)(2,1)S(1)} %get-tuple-element.14, bf16[2,512,2,1,512]{4,3,1,2,0:T(2,128)(2,1)S(1)} %get-tuple-element.13), kind=kLoop, calls=%fused_computation.33 | loop fusion | flops 8388608 | bytes 8388608 | tf_op jit(solution)/shard_map/stack | solution.py:33
  236.5 7.8 %stack.68 = bf16[2,1,4,128,2,1024]{5,3,2,4,0,1:T(8,128)(2,1)} reshape(bf16[2,512,2,2,512]{4,3,1,2,0:T(2,128)(2,1)} %pad_maximum_fusion.1) | data formatting | bytes 8388608 | tf_op jit(solution)/shard_map/stack | solution.py:34
  244.3 7.8 %stack.66 = bf16[2,1,4,128,2,1024]{5,3,2,4,0,1:T(8,128)(2,1)} reshape(bf16[2,512,2,2,512]{4,3,1,2,0:T(2,128)(2,1)} %collective-permute-done) | data formatting | bytes 8388608 | tf_op jit(solution)/shard_map/stack | solution.py:34
  252.1 8.2 %fusion.31 = bf16[4,4,2,128,2,128]{3,5,0,1,4,2:T(8,128)(2,1)S(1)} fusion(f32[]{:T(128)S(6)} %div.19, bf16[2,4,128,2,1024,1,1]{4,2,0,1,6,5,3:T(8,128)(2,1)} %copy-done.1, bf16[2,1,4,128,2,1024]{5,3,2,4,0,1:T(8,128)(2,1)} %stack.68, bf16[2,1,4,128,2,1024]{5,3,2,4,0,1:T(8,128)(2,1)} %stack.66), kind=kOutput, calls=%fused_computation.51 | convolution fusion | flops 4301258752 | bytes 14680068 | tf_op jit(solution)/shard_map/wqibk,wpsjbk->qsbipj/dot_general | solution.py:37
  260.3 0.1 copy.52
  260.5 1.4 constant_dynamic-update-slice_fusion.3
  261.9 10.9 %slice_negate_fusion.2 = (bf16[2,512,2,1,512]{4,3,1,2,0:T(2,128)(2,1)S(1)}, bf16[2,512,2,1,512]{4,3,1,2,0:T(2,128)(2,1)S(1)}) fusion(bf16[2,512,2,2,512]{4,3,1,2,0:T(2,128)(2,1)} %collective-permute-done.1), kind=kLoop, calls=%fused_computation.29 | loop fusion | flops 1048576 | bytes 8388608 | tf_op jit(solution)/shard_map/neg | solution.py:33
  272.8 10.6 %pad_maximum_fusion.2 = bf16[2,512,2,2,512]{4,3,1,2,0:T(2,128)(2,1)} fusion(bf16[2,512,2,1,512]{4,3,1,2,0:T(2,128)(2,1)S(1)} %get-tuple-element.12, bf16[2,512,2,1,512]{4,3,1,2,0:T(2,128)(2,1)S(1)} %get-tuple-element.11), kind=kLoop, calls=%fused_computation.34 | loop fusion | flops 8388608 | bytes 8388608 | tf_op jit(solution)/shard_map/stack | solution.py:33
  283.3 7.8 %stack.72 = bf16[2,1,4,128,2,1024]{5,3,2,4,0,1:T(8,128)(2,1)} reshape(bf16[2,512,2,2,512]{4,3,1,2,0:T(2,128)(2,1)} %pad_maximum_fusion.2) | data formatting | bytes 8388608 | tf_op jit(solution)/shard_map/stack | solution.py:34
  291.1 7.7 %stack.70 = bf16[2,1,4,128,2,1024]{5,3,2,4,0,1:T(8,128)(2,1)} reshape(bf16[2,512,2,2,512]{4,3,1,2,0:T(2,128)(2,1)} %collective-permute-done.1) | data formatting | bytes 8388608 | tf_op jit(solution)/shard_map/stack | solution.py:34
  298.8 4.1 collective-permute-done.2
  302.9 4.5 collective-permute-start.3
  307.4 8.2 %fusion.34 = bf16[4,4,2,128,2,128]{3,5,0,1,4,2:T(8,128)(2,1)S(1)} fusion(f32[]{:T(128)S(6)} %div.19, bf16[2,4,128,2,1024,1,1]{4,2,0,1,6,5,3:T(8,128)(2,1)} %copy-done.1, bf16[2,1,4,128,2,1024]{5,3,2,4,0,1:T(8,128)(2,1)} %stack.72, bf16[2,1,4,128,2,1024]{5,3,2,4,0,1:T(8,128)(2,1)} %stack.70), kind=kOutput, calls=%fused_computation.52 | convolution fusion | flops 4301258752 | bytes 14680068 | tf_op jit(solution)/shard_map/wqibk,wpsjbk->qsbipj/dot_general | solution.py:37
  315.7 0.1 copy.55
  315.8 1.5 constant_dynamic-update-slice_fusion.2
  317.3 10.9 %slice_negate_fusion.1 = (bf16[2,512,2,1,512]{4,3,1,2,0:T(2,128)(2,1)S(1)}, bf16[2,512,2,1,512]{4,3,1,2,0:T(2,128)(2,1)S(1)}) fusion(bf16[2,512,2,2,512]{4,3,1,2,0:T(2,128)(2,1)} %collective-permute-done.2), kind=kLoop, calls=%fused_computation.28 | loop fusion | flops 1048576 | bytes 8388608 | tf_op jit(solution)/shard_map/neg | solution.py:33
  328.1 10.5 %pad_maximum_fusion.3 = bf16[2,512,2,2,512]{4,3,1,2,0:T(2,128)(2,1)} fusion(bf16[2,512,2,1,512]{4,3,1,2,0:T(2,128)(2,1)S(1)} %get-tuple-element.10, bf16[2,512,2,1,512]{4,3,1,2,0:T(2,128)(2,1)S(1)} %get-tuple-element.9), kind=kLoop, calls=%fused_computation.35 | loop fusion | flops 8388608 | bytes 8388608 | tf_op jit(solution)/shard_map/stack | solution.py:33
  338.7 7.8 %stack.76 = bf16[2,1,4,128,2,1024]{5,3,2,4,0,1:T(8,128)(2,1)} reshape(bf16[2,512,2,2,512]{4,3,1,2,0:T(2,128)(2,1)} %pad_maximum_fusion.3) | data formatting | bytes 8388608 | tf_op jit(solution)/shard_map/stack | solution.py:34
  346.4 7.7 %stack.74 = bf16[2,1,4,128,2,1024]{5,3,2,4,0,1:T(8,128)(2,1)} reshape(bf16[2,512,2,2,512]{4,3,1,2,0:T(2,128)(2,1)} %collective-permute-done.2) | data formatting | bytes 8388608 | tf_op jit(solution)/shard_map/stack | solution.py:34
  354.2 8.2 %fusion.37 = bf16[4,4,2,128,2,128]{3,5,0,1,4,2:T(8,128)(2,1)S(1)} fusion(f32[]{:T(128)S(6)} %div.19, bf16[2,4,128,2,1024,1,1]{4,2,0,1,6,5,3:T(8,128)(2,1)} %copy-done.1, bf16[2,1,4,128,2,1024]{5,3,2,4,0,1:T(8,128)(2,1)} %stack.76, bf16[2,1,4,128,2,1024]{5,3,2,4,0,1:T(8,128)(2,1)} %stack.74), kind=kOutput, calls=%fused_computation.53 | convolution fusion | flops 4301258752 | bytes 14680068 | tf_op jit(solution)/shard_map/wqibk,wpsjbk->qsbipj/dot_general | solution.py:37
  362.4 0.1 copy.58
  362.6 1.5 constant_dynamic-update-slice_fusion.1
  364.0 30.4 %collective-permute-done.3 = bf16[2,512,2,2,512]{4,3,1,2,0:T(2,128)(2,1)} collective-permute-done((bf16[2,512,2,2,512]{4,3,1,2,0:T(2,128)(2,1)}, bf16[2,512,2,2,512]{4,3,1,2,0:T(2,128)(2,1)}, u32[]{:S(2)}, u32[]{:S(2)}) %collective-permute-start.3) | collective-permute-done | bytes 4194336 | tf_op jit(solution)/shard_map/ppermute | solution.py:17
  394.4 10.9 %slice_negate_fusion = (bf16[2,512,2,1,512]{4,3,1,2,0:T(2,128)(2,1)S(1)}, bf16[2,512,2,1,512]{4,3,1,2,0:T(2,128)(2,1)S(1)}) fusion(bf16[2,512,2,2,512]{4,3,1,2,0:T(2,128)(2,1)} %collective-permute-done.3), kind=kLoop, calls=%fused_computation.27 | loop fusion | flops 1048576 | bytes 8388608 | tf_op jit(solution)/shard_map/neg | solution.py:33
  405.3 10.5 %pad_maximum_fusion.4 = bf16[2,512,2,2,512]{4,3,1,2,0:T(2,128)(2,1)} fusion(bf16[2,512,2,1,512]{4,3,1,2,0:T(2,128)(2,1)S(1)} %get-tuple-element.8, bf16[2,512,2,1,512]{4,3,1,2,0:T(2,128)(2,1)S(1)} %get-tuple-element.7), kind=kLoop, calls=%fused_computation.36 | loop fusion | flops 8388608 | bytes 8388608 | tf_op jit(solution)/shard_map/stack | solution.py:33
  415.9 7.7 %stack.80 = bf16[2,1,4,128,2,1024]{5,3,2,4,0,1:T(8,128)(2,1)} reshape(bf16[2,512,2,2,512]{4,3,1,2,0:T(2,128)(2,1)} %pad_maximum_fusion.4) | data formatting | bytes 8388608 | tf_op jit(solution)/shard_map/stack | solution.py:34
  423.6 7.8 %stack.78 = bf16[2,1,4,128,2,1024]{5,3,2,4,0,1:T(8,128)(2,1)} reshape(bf16[2,512,2,2,512]{4,3,1,2,0:T(2,128)(2,1)} %collective-permute-done.3) | data formatting | bytes 8388608 | tf_op jit(solution)/shard_map/stack | solution.py:34
  431.3 8.5 %fusion.40 = bf16[4,4,2,128,2,128]{3,5,0,1,4,2:T(8,128)(2,1)S(1)} fusion(f32[]{:T(128)S(6)} %div.19, bf16[2,4,128,2,1024,1,1]{4,2,0,1,6,5,3:T(8,128)(2,1)} %copy-done.1, bf16[2,1,4,128,2,1024]{5,3,2,4,0,1:T(8,128)(2,1)} %stack.80, bf16[2,1,4,128,2,1024]{5,3,2,4,0,1:T(8,128)(2,1)} %stack.78), kind=kOutput, calls=%fused_computation.54 | convolution fusion | flops 4301258752 | bytes 14680068 | tf_op jit(solution)/shard_map/wqibk,wpsjbk->qsbipj/dot_general | solution.py:37
  439.8 0.1 copy.61
  440.0 1.5 constant_dynamic-update-slice_fusion
  441.5 12.1 %gather_fusion = bf16[128,2,128,256]{2,3,1,0:T(8,128)(2,1)} fusion(bf16[80,2,128,256]{2,3,1,0:T(8,128)(2,1)} %constant_dynamic-update-slice_fusion, s32[1024]{0:T(1024)S(1)} %pad_clamp_fusion), kind=kCustom, calls=%fused_computation | custom fusion | bytes 33554944 | tf_op jit(solution)/shard_map/jit(_take)/gather | solution.py:84
  453.6 14.3 %select_select_fusion = bf16[16,8,2,128,256]{3,4,2,1,0:T(8,128)(2,1)} fusion(bf16[16,8,2,128,256]{3,4,2,1,0:T(8,128)(2,1)} %bitcast.133, pred[16,8]{1,0:T(8,128)(4,1)S(1)} %compare_and_fusion, pred[16,8]{1,0:T(8,128)(4,1)S(1)} %broadcast_in_dim.54), kind=kLoop, calls=%fused_computation.1 | loop fusion | flops 16777216 | bytes 33554688 | tf_op jit(solution)/shard_map/jit(_where)/select_n | solution.py:85
  467.9 11.6 %all-to-all-start = ((bf16[16,8,2,128,256]{3,4,2,1,0:T(8,128)(2,1)}), bf16[16,8,2,128,256]{3,4,2,1,0:T(8,128)(2,1)}, u32[]{:S(2)}, u32[]{:S(2)}) async-start(bf16[16,8,2,128,256]{3,4,2,1,0:T(8,128)(2,1)} %select_select_fusion), calls=%async_computation | async-start | bytes 33554432 | tf_op jit(solution)/shard_map/all_to_all | solution.py:88
  479.5 0.9 multiply_convert_fusion.2
  480.4 0.9 fusion.57
  481.2 268.1 %all-to-all-done = bf16[16,8,2,128,256]{3,4,2,1,0:T(8,128)(2,1)} async-done(((bf16[16,8,2,128,256]{3,4,2,1,0:T(8,128)(2,1)}), bf16[16,8,2,128,256]{3,4,2,1,0:T(8,128)(2,1)}, u32[]{:S(2)}, u32[]{:S(2)}) %all-to-all-start) | async-done | bytes 16777248 | tf_op jit(solution)/shard_map/all_to_all | solution.py:88
  749.3 8.9 %reduce_sum.60 = bf16[8,2,128,256]{2,3,1,0:T(8,128)(2,1)S(1)} reduce(bf16[16,8,2,128,256]{3,4,2,1,0:T(8,128)(2,1)} %all-to-all-done, bf16[]{:T(256)} %constant.40.clone.1), dimensions={0}, to_apply=%region_4.5 | reduce | flops 7864320 | bytes 17825794 | tf_op jit(solution)/shard_map/reduce_sum | solution.py:87
  758.2 0.8 multiply_bitcast_fusion
  759.0 0.3 fusion.29
  759.3 0.6 copy.63
  (18 shorter events, 0.4 us)
Async XLA Ops:
  22.6 94.5 %collective-permute-start = (bf16[2,512,2,2,512]{4,3,1,2,0:T(2,128)(2,1)}, bf16[2,512,2,2,512]{4,3,1,2,0:T(2,128)(2,1)}, u32[]{:S(2)}, u32[]{:S(2)}) collective-permute-start(bf16[2,512,2,2,512]{4,3,1,2,0:T(2,128)(2,1)} %fusion.14), channel_id=1, source_target_pairs={{0,112},{16,0},{32,16},{48,32},{64,48},{80,64},{96,80},{112,96},{1... | collective-permute-start | bytes 12582920 | tf_op jit(solution)/shard_map/ppermute | solution.py:17
  117.0 93.5 %collective-permute-start.1 = (bf16[2,512,2,2,512]{4,3,1,2,0:T(2,128)(2,1)}, bf16[2,512,2,2,512]{4,3,1,2,0:T(2,128)(2,1)}, u32[]{:S(2)}, u32[]{:S(2)}) collective-permute-start(bf16[2,512,2,2,512]{4,3,1,2,0:T(2,128)(2,1)} %collective-permute-done), channel_id=1, source_target_pairs={{0,112},{16,0},{32,16},{48,32},{64,48},{80,64},{96,80},{112,96},{1... | collective-permute-start | bytes 12582920 | tf_op jit(solution)/shard_map/ppermute | solution.py:17
  150.1 6.8 copy-start
  156.9 2.1 copy-start.1
  156.9 3.7 copy-start.2
  165.4 0.7 copy-start.4
  210.6 92.3 %collective-permute-start.2 = (bf16[2,512,2,2,512]{4,3,1,2,0:T(2,128)(2,1)}, bf16[2,512,2,2,512]{4,3,1,2,0:T(2,128)(2,1)}, u32[]{:S(2)}, u32[]{:S(2)}) collective-permute-start(bf16[2,512,2,2,512]{4,3,1,2,0:T(2,128)(2,1)} %collective-permute-done.1), channel_id=1, source_target_pairs={{0,112},{16,0},{32,16},{48,32},{64,48},{80,64},{96,80},{112,96},{1... | collective-permute-start | bytes 12582920 | tf_op jit(solution)/shard_map/ppermute | solution.py:17
  302.9 91.5 %collective-permute-start.3 = (bf16[2,512,2,2,512]{4,3,1,2,0:T(2,128)(2,1)}, bf16[2,512,2,2,512]{4,3,1,2,0:T(2,128)(2,1)}, u32[]{:S(2)}, u32[]{:S(2)}) collective-permute-start(bf16[2,512,2,2,512]{4,3,1,2,0:T(2,128)(2,1)} %collective-permute-done.2), channel_id=1, source_target_pairs={{0,112},{16,0},{32,16},{48,32},{64,48},{80,64},{96,80},{112,96},{1... | collective-permute-start | bytes 12582920 | tf_op jit(solution)/shard_map/ppermute | solution.py:17
  467.9 11.6 %copy-start.3 = (f32[2,128,256]{2,1,0:T(8,128)S(1)}, f32[2,128,256]{2,1,0:T(8,128)}, u32[]{:S(2)}) copy-start(f32[2,128,256]{2,1,0:T(8,128)} %param.7) | copy-start | bytes 786436
  467.9 281.4 %all-to-all-start = ((bf16[16,8,2,128,256]{3,4,2,1,0:T(8,128)(2,1)}), bf16[16,8,2,128,256]{3,4,2,1,0:T(8,128)(2,1)}, u32[]{:S(2)}, u32[]{:S(2)}) async-start(bf16[16,8,2,128,256]{3,4,2,1,0:T(8,128)(2,1)} %select_select_fusion), calls=%async_computation | async-start | bytes 33554432 | tf_op jit(solution)/shard_map/all_to_all | solution.py:88
where the time goes:
time: 768 us; the launch traced here: 760 us
  waiting for transfers between devices  392 us (51%)
  other arithmetic  151 us (20%)
  local copies, waits for them, and re-layouts  147 us (19%)
  matrix products  38.7 us (5%)
  starting transfers between devices  30.2 us (4%)
    all_to_all x1, waiting for transfers between devices, body(): lax.all_to_all(outgoing, 'seg', split_axis=0, concat_axis=0, tiled=True)  268 us
    ppermute x4, waiting for transfers between devices, from_behind(): lax.ppermute(array, axis, [(i, (i + by) % devices) for i in range(devices)])  124 us
    another operation x9, local copies, waits for them, and re-layouts, correlate(): both_parts = jnp.stack([visiting, flipped], axis=1)  69.7 us
    neg x5, other arithmetic, correlate(): flipped = jnp.stack([-visiting[:, :, :, 1], visiting[:, :, :, 0]], axis=3)  54.5 us
    convert_element_type x4, local copies, waits for them, and re-layouts, prepare(): segment_data.astype(jnp.float32).reshape(windows, channels, BANDS, 2, FB)  52.7 us
    another operation x5, other arithmetic, correlate(): flipped = jnp.stack([-visiting[:, :, :, 1], visiting[:, :, :, 0]], axis=3)  52.6 us
    dot_general x5, matrix products, correlate(): jnp.einsum('wqibk,wpsjbk->qsbipj', left_side, right_side, preferred_eleme...  38 us
    ppermute x4, starting transfers between devices, from_behind(): lax.ppermute(array, axis, [(i, (i + by) % devices) for i in range(devices)])  18.7 us
  transfers between devices with their start and end apart: 5, of which 5 were waited for; matrix products, arithmetic and copies ran while one was open for 30% of the time, Pallas kernels for 0%

commit v1 on v0

v1 whole, which is shorter than its diff:
```python
import math

import jax
import jax.numpy as jnp
from jax import lax
from jax.experimental import pallas as pl
from jax.experimental.pallas import tpu as pltpu
from jax.sharding import PartitionSpec as P

TILE = 128
BANDS = 2
CAP = 8
FB = 512
QUAD = 4
ROUNDS = 10
PART = 2 * FB
MESH = pl.DeviceIdType.MESH


def pick(index, values):
    total = 0
    for key, value in enumerate(values):
        total = total + jnp.where(index == key, value, 0)
    return total


def kernel(
    rows_ref, filled_ref, scale_ref, spectra_ref, phases_ref, out_ref,
    raw, zs, data, out, core_in, relay_in, ring_in, zhi_in, zhi_out, keep,
    phase, matrix, powers, gathered,
    raw_sem, phase_sem, z_sem, up_sem, dn_sem, core_sem, relay_sem, ring_sem, zhi_sem,
    near_send, near_recv, far_send, far_recv,
):
    blk = lax.axis_index("blk")
    seg = lax.axis_index("seg")
    y, zl = blk // 2, blk % 2
    x, zh, core = seg // 4, (seg // 2) % 2, seg % 2
    first, second = zl, 1 - zl
    left, right = (x + 3) % 4, (x + 1) % 4

    def seat(nx, nzh, nc):
        return nx * 4 + nzh * 2 + nc

    def remote(src, dst, sems, index, device):
        return pltpu.make_async_remote_copy(
            src_ref=src, dst_ref=dst,
            send_sem=sems.at[(0,) + index], recv_sem=sems.at[(1,) + index],
            device_id=device, device_id_type=MESH,
        )

    def z_copy(j):
        return remote(zs.at[j], data.at[2 * zl, j], z_sem, (j,), (2 * y + 1 - zl, seg))

    def z_wait(j):
        remote(zs.at[j], data.at[2 * second, j], z_sem, (j,), (2 * y + 1 - zl, seg)).wait_recv()

    def up_copy(p, j):
        return remote(data.at[2 * p, j], data.at[8 + p, j], up_sem, (p, j), (2 * ((y + 3) % 4) + zl, seg))

    def dn_copy(p, j):
        return remote(data.at[2 * p, j], data.at[4 + 2 * p, j], dn_sem, (p, j), (2 * ((y + 1) % 4) + zl, seg))

    def core_copy(n):
        return remote(
            out.at[n, pl.ds(2 * (1 - core), 2)], core_in.at[n], core_sem, (n,),
            (blk, seat(x, zh, 1 - core)),
        )

    def relay_copy(n, side):
        return remote(
            out.at[n, 2 * core + side, (x + 2) % 4], relay_in.at[n, side], relay_sem, (n, side),
            (blk, seat(right if side else left, zh, core)),
        )

    def ring_copy(n, side):
        to = right if side else left
        return remote(
            out.at[n, pl.ds(2 * core, 2), to], ring_in.at[n, side], ring_sem, (n, side),
            (blk, seat(to, zh, core)),
        )

    def zhi_copy(n):
        return remote(zhi_out.at[n], zhi_in.at[n], zhi_sem, (n,), (blk, seat(x, 1 - zh, core)))

    me = zl * 16 + seg

    def near_copy(i):
        return pltpu.make_async_remote_copy(
            src_ref=powers.at[pl.ds(0, 8)],
            dst_ref=gathered.at[pl.ds(pl.multiple_of(me * 8, 8), 8)],
            send_sem=near_send.at[i], recv_sem=near_recv.at[me],
            device_id=(2 * y + (zl + i // 16) % 2, (seg + i % 16) % 16), device_id_type=MESH,
        )

    def near_wait(i):
        other = ((zl + i // 16) % 2) * 16 + (seg + i % 16) % 16
        pltpu.make_async_remote_copy(
            src_ref=powers.at[pl.ds(0, 8)],
            dst_ref=gathered.at[pl.ds(pl.multiple_of(other * 8, 8), 8)],
            send_sem=near_send.at[i], recv_sem=near_recv.at[other],
            device_id=(2 * y + (zl + i // 16) % 2, (seg + i % 16) % 16), device_id_type=MESH,
        ).wait_recv()

    def far_copy(i):
        return pltpu.make_async_remote_copy(
            src_ref=powers.at[pl.ds(8, 8)],
            dst_ref=gathered.at[pl.ds(pl.multiple_of((32 + me) * 8, 8), 8)],
            send_sem=far_send.at[i], recv_sem=far_recv.at[me],
            device_id=(2 * ((y + 3) % 4) + (zl + i // 16) % 2, (seg + i % 16) % 16),
            device_id_type=MESH,
        )

    def far_wait(i):
        pltpu.make_async_remote_copy(
            src_ref=powers.at[pl.ds(8, 8)],
            dst_ref=gathered.at[pl.ds(pl.multiple_of((32 + i) * 8, 8), 8)],
            send_sem=far_send.at[i], recv_sem=far_recv.at[i],
            device_id=(2 * ((y + 3) % 4) + i // 16, i % 16), device_id_type=MESH,
        ).wait_recv()

    def each(count, action):
        def step(i, carry):
            action(i)
            return carry

        lax.fori_loop(0, count, step, 0)

    def raw_copy(j):
        return pltpu.make_async_copy(
            spectra_ref.at[:, pl.ds(pl.multiple_of(j * TILE, TILE), TILE), :], raw.at[j], raw_sem.at[j]
        )

    phase_copy = pltpu.make_async_copy(phases_ref.at[zl], phase, phase_sem.at[0])
    for j in range(QUAD):
        raw_copy(j).start()
    phase_copy.start()

    def whiten(j):
        raw_copy(j).wait()

        def some_rows(r):
            rows = pl.ds(pl.multiple_of(r * 16, 16), 16)
            for w in range(2):
                mine = raw[j, w, rows, pl.ds(pl.multiple_of(zl * PART, PART), PART)].astype(jnp.float32)
                theirs = raw[j, w, rows, pl.ds(pl.multiple_of(second * PART, PART), PART)].astype(jnp.float32)
                square = jnp.sum(mine * mine + theirs * theirs, axis=1, keepdims=True)
                scaling = lax.rsqrt(square * (1.0 / (2 * PART)) + 1e-05) * scale_ref[1 + w]
                mine = (mine * scaling).astype(jnp.bfloat16)
                data[2 * zl, j, rows, w * PART : (w + 1) * PART] = mine
                data[2 * zl + 1, j, rows, w * PART : w * PART + FB] = mine[:, FB:]
                data[2 * zl + 1, j, rows, w * PART + FB : (w + 1) * PART] = -mine[:, :FB]
                zs[j, rows, w * PART : (w + 1) * PART] = (theirs * scaling).astype(jnp.bfloat16)

        each(TILE // 16, some_rows)
        z_copy(j).start()
        up_copy(zl, j).start()
        dn_copy(zl, j).start()

    each(QUAD, whiten)

    def flip(slab, j):
        def some_rows(r):
            rows = pl.ds(pl.multiple_of(r * 16, 16), 16)
            for w in range(2):
                data[slab + 1, j, rows, w * PART : w * PART + FB] = data[slab, j, rows, w * PART + FB : (w + 1) * PART]
                data[slab + 1, j, rows, w * PART + FB : (w + 1) * PART] = -data[slab, j, rows, w * PART : w * PART + FB]

        each(TILE // 16, some_rows)

    phase_copy.wait()
    angles = phase[...]
    norm_factor = 1.0 / math.sqrt(TILE)
    cosine = (jnp.cos(angles) * norm_factor).astype(jnp.bfloat16)
    sine_part = (jnp.sin(angles) * norm_factor).astype(jnp.bfloat16)
    velocities = angles.shape[1]
    matrix[:TILE, :velocities] = cosine
    matrix[:TILE, velocities:] = sine_part
    matrix[TILE:, :velocities] = -sine_part
    matrix[TILE:, velocities:] = cosine
    powers[...] = jnp.zeros_like(powers)

    def job(n, h):
        @pl.when(n == 1)
        def _():
            for jj in range(2):
                j = 2 * h + jj
                z_wait(j)
                up_copy(second, j).start()
                dn_copy(second, j).start()
                flip(2 * second, j)
                up_copy(first, j).wait_recv()
                dn_copy(first, j).wait_recv()
                flip(4 + 2 * first, j)

        @pl.when(((n == 6) | (n == 7)) & (h == 0))
        def _():
            for jj in range(2):
                j = 2 * (n - 6) + jj
                up_copy(second, j).wait_recv()
                dn_copy(second, j).wait_recv()
                flip(4 + 2 * second, j)

        either = (zl + h) % 2
        left_slab = pick(n, [first, first, second, 0, second, 2 + first, either, either, 2 + second, 3])
        right_slab = pick(
            n, [2 * first, 8 + first, 2 * second, 2, 8 + first, 8 + first, 8 + second, 8 + second, 8 + second, 8]
        )
        pair = pick(n, [h, h, h, h, h, h, 0, 1, h, h])
        left_side = data[pl.ds(2 * left_slab, 2)].reshape(2 * QUAD * TILE, 2 * PART)
        right_side = data[right_slab, pl.ds(2 * pair, 2)].reshape(2 * TILE, 2 * PART)
        product = lax.dot_general(
            left_side, right_side, (((1,), (1,)), ((), ())), preferred_element_type=jnp.float32
        )
        product = (product * scale_ref[0]).astype(jnp.bfloat16).reshape(2, QUAD, TILE, 2 * TILE)
        for jj in range(2):
            columns = slice(jj * TILE, (jj + 1) * TILE)
            out[n, 2 * h + jj, :, :, :TILE] = product[0, :, :, columns]
            out[n, 2 * h + jj, :, :, TILE:] = product[1, :, :, columns]

    def add_cores(n):
        core_copy(n).wait_recv()

        def one(t):
            q, r = t // 4, t % 4
            total = out[n, 2 * core + q, r].astype(jnp.float32) + core_in[n, q, r].astype(jnp.float32)
            out[n, 2 * core + q, r] = total.astype(jnp.bfloat16)

        each(8, one)
        for side in range(2):
            relay_copy(n, side).start()

    def add_relayed(n):
        for side in range(2):
            to = right if side else left
            relay_copy(n, side).wait_recv()
            total = out[n, 2 * core + side, to].astype(jnp.float32) + relay_in[n, side].astype(jnp.float32)
            out[n, 2 * core + side, to] = total.astype(jnp.bfloat16)
        for side in range(2):
            ring_copy(n, side).start()

    def add_ring(n):
        for side in range(2):
            ring_copy(n, side).wait_recv()

        def total(z):
            return (
                out[n, 2 * core + z, x].astype(jnp.float32)
                + ring_in[n, 0, z].astype(jnp.float32)
                + ring_in[n, 1, z].astype(jnp.float32)
            )

        zhi_out[n] = total(1 - zh).astype(jnp.bfloat16)
        zhi_copy(n).start()
        keep[n] = total(zh)

    def add_last(n):
        zhi_copy(n).wait_recv()
        stacked = (keep[n] + zhi_in[n].astype(jnp.float32)).astype(jnp.bfloat16)
        field = jnp.dot(stacked, matrix[...], preferred_element_type=jnp.float32)
        squared = field * field
        energy = squared[:, :velocities] + squared[:, velocities:]
        power = jnp.sum(energy, axis=0, keepdims=True) * (1.0 / TILE)
        powers[pl.ds(n, 1), :] = power

        @pl.when(n == 5)
        def _():
            powers[10:11, :] = power

    def step(n):
        @pl.when(n < ROUNDS)
        def _():
            each(2, lambda h: job(n, h))
            core_copy(n).start()

        @pl.when((n >= 1) & (n <= ROUNDS))
        def _():
            add_cores(n - 1)

        @pl.when((n >= 2) & (n <= ROUNDS + 1))
        def _():
            add_relayed(n - 2)

        @pl.when((n >= 3) & (n <= ROUNDS + 2))
        def _():
            add_ring(n - 3)

        @pl.when(n >= 4)
        def _():
            add_last(n - 4)

    each(ROUNDS + 4, step)

    gathered[pl.ds(pl.multiple_of(me * 8, 8), 8), :] = powers[:8, :]
    each(31, lambda i: near_copy(i + 1).start())
    each(32, lambda i: far_copy(i).start())
    each(31, lambda i: near_wait(i + 1))
    each(32, far_wait)

    for c in range(CAP):
        for g in range(BANDS):
            row = gathered[pl.ds(rows_ref[c * BANDS + g], 1), :]
            out_ref[c, g : g + 1, :] = jnp.where(filled_ref[c] > 0, row, jnp.zeros_like(row))

    def drain_exchange(j):
        z_copy(j).wait_send()
        for p in range(2):
            up_copy(p, j).wait_send()
            dn_copy(p, j).wait_send()

    each(QUAD, drain_exchange)

    def drain_rounds(n):
        core_copy(n).wait_send()
        for side in range(2):
            relay_copy(n, side).wait_send()
            ring_copy(n, side).wait_send()
        zhi_copy(n).wait_send()

    each(ROUNDS, drain_rounds)
    each(31, lambda i: near_copy(i + 1).wait_send())
    each(32, lambda i: far_copy(i).wait_send())


def slot_rows(owner_row, block, segment):
    count_tiles = owner_row.shape[0]
    order_ids = jnp.arange(count_tiles, dtype=jnp.int32)
    mine = owner_row == segment
    earlier = order_ids[None, :] < order_ids[:, None]
    rank_of = jnp.sum(jnp.where(mine[None, :] & earlier, 1, 0), axis=1).astype(jnp.int32)
    slots = jnp.arange(CAP, dtype=jnp.int32)
    matches = mine[None, :] & (rank_of[None, :] == slots[:, None])
    tile = jnp.sum(jnp.where(matches, order_ids[None, :], 0), axis=1)[:, None]
    filled = jnp.sum(jnp.where(matches, 1, 0), axis=1).astype(jnp.int32)
    band = jnp.arange(BANDS, dtype=jnp.int32)[None, :]
    parity = block % 2
    k, p, q = tile // 16, (tile // 4) % 4, tile % 4
    reach = parity + k
    apart = reach // 2
    row_first = parity == band
    column_first = reach % 2 == band
    both = row_first & column_first
    neither = ~row_first & ~column_first
    within = jnp.where(both, 0, jnp.where(neither, 2, 3))
    beside = jnp.where(both, 1, jnp.where(column_first, 4, 6 + q // 2))
    across = jnp.where(both, 2, jnp.where(neither, 0, 1))
    place = jnp.where(apart == 0, within, jnp.where(apart == 1, beside, across))
    late = (apart == 1) & ~column_first
    core = jnp.where(late, jnp.where(row_first, 0, 1), q // 2)
    source = band * 16 + p * 4 + (q % 2) * 2 + core + jnp.where(apart == 2, 32, 0)
    return (source * 8 + place).reshape(-1).astype(jnp.int32), filled


def body(spectra, window_count, tile_owner, phases):
    counted = window_count[0]
    windows = spectra.shape[1]
    velocities = phases.shape[2]
    weight = 1.0 / (counted.astype(jnp.float32) * math.sqrt(FB * lax.axis_size("seg")))
    live = (jnp.arange(windows, dtype=jnp.int32) < counted).astype(jnp.float32)
    scale = jnp.concatenate([weight[None], live])
    rows, filled = slot_rows(tile_owner[0], lax.axis_index("blk"), lax.axis_index("seg"))
    bf16, f32 = jnp.bfloat16, jnp.float32
    dma = pltpu.SemaphoreType.DMA
    response = pl.pallas_call(
        kernel,
        out_shape=jax.ShapeDtypeStruct((CAP, BANDS, velocities), f32),
        in_specs=[pl.BlockSpec(memory_space=pltpu.SMEM)] * 3 + [pl.BlockSpec(memory_space=pl.ANY)] * 2,
        out_specs=pl.BlockSpec(memory_space=pltpu.VMEM),
        scratch_shapes=[
            pltpu.VMEM((QUAD, 2, TILE, 2 * PART), bf16),
            pltpu.VMEM((QUAD, TILE, 2 * PART), bf16),
            pltpu.VMEM((10, QUAD, TILE, 2 * PART), bf16),
            pltpu.VMEM((ROUNDS, 4, QUAD, TILE, 2 * TILE), bf16),
            pltpu.VMEM((ROUNDS, 2, QUAD, TILE, 2 * TILE), bf16),
            pltpu.VMEM((ROUNDS, 2, TILE, 2 * TILE), bf16),
            pltpu.VMEM((ROUNDS, 2, 2, TILE, 2 * TILE), bf16),
            pltpu.VMEM((ROUNDS, TILE, 2 * TILE), bf16),
            pltpu.VMEM((ROUNDS, TILE, 2 * TILE), bf16),
            pltpu.VMEM((ROUNDS, TILE, 2 * TILE), f32),
            pltpu.VMEM((TILE, velocities), f32),
            pltpu.VMEM((2 * TILE, 2 * velocities), bf16),
            pltpu.VMEM((16, velocities), f32),
            pltpu.VMEM((64 * 8, velocities), f32),
            dma((QUAD,)),
            dma((1,)),
            dma((2, QUAD)),
            dma((2, 2, QUAD)),
            dma((2, 2, QUAD)),
            dma((2, ROUNDS)),
            dma((2, ROUNDS, 2)),
            dma((2, ROUNDS, 2)),
            dma((2, ROUNDS)),
            dma((32,)),
            dma((32,)),
            dma((32,)),
            dma((32,)),
        ],
        compiler_params=pltpu.CompilerParams(vmem_limit_bytes=60 * 1024 * 1024, has_side_effects=True),
    )(rows, filled, scale, spectra[0], phases)
    return response[None, None]


def solution(mesh):
    placed = (P("seg", None, "blk", None), P("seg"), P("blk", None), P())
    return jax.shard_map(
        body,
        mesh=mesh,
        in_specs=placed,
        out_specs=P("blk", "seg", None, None, None),
        check_vma=False,
    )
```

time: 768 us -> 156 us (0.20); the launches traced: 760 us -> 156 us
  waiting for transfers between devices: 392 us -> 0 us
  Pallas kernels: 0 us -> 150 us
  other arithmetic: 151 us -> 2.85 us
  local copies, waits for them, and re-layouts: 147 us -> 2.47 us
  matrix products: 38.7 us -> 0 us
  starting transfers between devices: 30.2 us -> 0 us
    all_to_all x1 -> x0, waiting for transfers between devices: 268 us -> none  [body(): lax.all_to_all(outgoing, 'seg', split_axis=0, concat_axis=0, tiled=True)]
    pallas_call x0 -> x1, Pallas kernels: none -> 150 us  [body(): pl.pallas_call(kernel, out_shape=jax.ShapeDtypeStruct((CAP, BANDS, veloci...]
    ppermute x4 -> x0, waiting for transfers between devices: 124 us -> none  [from_behind(): lax.ppermute(array, axis, [(i, (i + by) % devices) for i in range(devices)])]
    another operation x9 -> x0, local copies, waits for them, and re-layouts: 69.7 us -> none  [correlate(): both_parts = jnp.stack([visiting, flipped], axis=1)]
    neg x6 -> x0, other arithmetic: 55.4 us -> none  [the longest x5 54.5 us: correlate(): flipped = jnp.stack([-visiting[:, :, :, 1], visiting[:, :, :, 0]], axis=3)]
    convert_element_type x9 -> x0, local copies, waits for them, and re-layouts: 53.4 us -> none  [the longest x4 52.7 us: prepare(): segment_data.astype(jnp.float32).reshape(windows, channels, BANDS, 2, FB)]
    another operation x5 -> x0, other arithmetic: 52.6 us -> none  [correlate(): flipped = jnp.stack([-visiting[:, :, :, 1], visiting[:, :, :, 0]], axis=3)]
    dot_general x6 -> x0, matrix products: 38.7 us -> none  [the longest x5 38 us: correlate(): jnp.einsum('wqibk,wpsjbk->qsbipj', left_side, right_side, preferred_eleme...]
  transfers between devices with their start and end apart: 5 -> 0, of which waited for: 5 -> 0; matrix products, arithmetic and copies ran while one was open for 30% -> 0% of each run, Pallas kernels for 0% -> 0%
where the time goes in v1:
time: 156 us
  Pallas kernels  150 us (96%)
  other arithmetic  2.85 us (2%)
  local copies, waits for them, and re-layouts  2.47 us (2%)
    pallas_call x1, Pallas kernels, body(): pl.pallas_call(kernel, out_shape=jax.ShapeDtypeStruct((CAP, BANDS, veloci...  150 us

profile of v1, /device:TPU:1, one launch (start us, length us, event | category | flops | bytes accessed | tf_op | source)
XLA Modules:
  0.0 156.3 jit_solution(17207654229065720710)
XLA Ops:
  0.7 0.7 compare_bitcast_fusion
  1.4 0.1 select_reduce_fusion
  1.5 0.6 select_reduce_fusion.1
  2.1 0.6 pad_maximum_fusion.scale_ref
  2.7 0.1 and.233
  2.8 0.1 and.224
  2.9 0.1 and.225
  3.0 0.1 broadcast_in_dim.133
  3.1 0.1 broadcast_in_dim.134
  3.2 0.1 fusion.3
  3.3 0.1 not.17
  3.4 0.1 and.231
  3.5 0.1 add_add_fusion
  3.5 0.1 add.172
  3.6 0.1 fusion.1
  3.7 0.1 select_n.197
  3.8 0.1 broadcast_in_dim.129
  3.9 0.1 broadcast_in_dim.130
  3.9 0.1 broadcast_in_dim.131
  4.0 0.1 add.178
  4.1 0.1 add.179
  4.2 0.6 select_add_fusion.rows_ref
  4.7 150.2 %shard_map.46 = f32[8,2,256]{2,1,0:T(2,128)} custom-call(s32[16]{0:T(128)} %select_add_fusion.rows_ref, s32[8]{0:T(128)} %get-tuple-element.5.filled_ref, f32[3]{0:T(128)} %pad_maximum_fusion.scale_ref, bf16[2,512,2048]{2,1,0:T(8,128)(2,1)} %bitcast.8, f32[2,128,256]{2,1,0:T(8,128)} %phases_ref.1), custom_call_target="tpu_custom_call" | custom-call | tf_op jit(solution)/shard_map/pallas_call | solution.py:363
  154.9 1.3 copy.7
  (10 shorter events, 0.1 us)

commit v2 on v1

v2 whole, which is shorter than its diff:
```python
import math

import jax
import jax.numpy as jnp
from jax import lax
from jax.experimental import pallas as pl
from jax.experimental.pallas import tpu as pltpu
from jax.sharding import PartitionSpec as P

TILE = 128
BANDS = 2
CAP = 8
FB = 512
QUAD = 4
ROUNDS = 10
NEAR_ROUNDS, WHOLE_ROUNDS = 5, 6
PART = 2 * FB
MESH = pl.DeviceIdType.MESH


def pick(index, values):
    total = 0
    for key, value in enumerate(values):
        total = total + jnp.where(index == key, value, 0)
    return total


def kernel(
    place_of, count_ref, spectra_ref, phases_ref, out_ref,
    raw, zs, data, out, core_in, relay_in, ring_in, zhi_in, zhi_out, keep,
    phase, matrix, column, powers, late_powers, turned_powers, near, far, late,
    raw_sem, phase_sem, z_sem, up_sem, dn_sem, core_sem, relay_sem, ring_sem, zhi_sem,
    near_sem, far_sem, late_sem, token, token_up, token_dn,
):
    blk = lax.axis_index("blk")
    seg = lax.axis_index("seg")
    y, zl = blk // 2, blk % 2
    x, zh, core = seg // 4, (seg // 2) % 2, seg % 2
    first, second = zl, 1 - zl
    left, right = (x + 3) % 4, (x + 1) % 4

    def seat(nx, nzh, nc):
        return nx * 4 + nzh * 2 + nc

    z_mate = (2 * y + 1 - zl, seg)
    y_down, y_up = (2 * ((y + 3) % 4) + zl, seg), (2 * ((y + 1) % 4) + zl, seg)
    core_mate, zhi_mate = (blk, seat(x, zh, 1 - core)), (blk, seat(x, 1 - zh, core))
    x_mates = (blk, seat(left, zh, core)), (blk, seat(right, zh, core))
    barrier = pltpu.get_barrier_semaphore()
    for mate in (z_mate, y_down, y_up, core_mate, zhi_mate, *x_mates):
        pl.semaphore_signal(barrier, inc=1, device_id=mate, device_id_type=MESH)

    def remote(src, dst, sems, index, device):
        return pltpu.make_async_remote_copy(
            src_ref=src, dst_ref=dst,
            send_sem=sems.at[(0,) + index], recv_sem=sems.at[(1,) + index],
            device_id=device, device_id_type=MESH,
        )

    def z_copy(j):
        return remote(zs.at[j], data.at[2 * zl, j], z_sem, (j,), z_mate)

    def z_wait(j):
        remote(zs.at[j], data.at[2 * second, j], z_sem, (j,), z_mate).wait_recv()

    def up_copy(p, j):
        return remote(data.at[2 * p, j], data.at[8 + p, j], up_sem, (p, j), y_down)

    def dn_copy(p, j):
        return remote(data.at[2 * p, j], data.at[4 + 2 * p, j], dn_sem, (p, j), y_up)

    def core_copy(n):
        return remote(
            out.at[n, pl.ds(2 * (1 - core), 2)], core_in.at[n], core_sem, (n,), core_mate
        )

    def relay_copy(n, side):
        return remote(
            out.at[n, 2 * core + side, (x + 2) % 4], relay_in.at[n, side], relay_sem, (n, side),
            x_mates[side],
        )

    def ring_copy(n, side):
        to = right if side else left
        return remote(
            out.at[n, pl.ds(2 * core, 2), to], ring_in.at[n, side], ring_sem, (n, side),
            x_mates[side],
        )

    def zhi_copy(n):
        return remote(zhi_out.at[n], zhi_in.at[n], zhi_sem, (n,), zhi_mate)

    def back(i):
        return (i // 16) * 16 + (16 - i % 16) % 16

    def gather_copy(source, target, sems, sent, filed, plane, i):
        device = (2 * ((y + plane) % 4) + (zl + i // 16) % 2, (seg + i % 16) % 16)
        return pltpu.make_async_remote_copy(
            src_ref=source, dst_ref=target.at[filed],
            send_sem=sems.at[0, sent], recv_sem=sems.at[1, filed],
            device_id=device, device_id_type=MESH,
        )

    def near_copy(i, filed):
        return gather_copy(powers.at[pl.ds(0, NEAR_ROUNDS)], near, near_sem, i, filed, 0, i)

    def far_copy(i, filed):
        return gather_copy(powers.at[pl.ds(NEAR_ROUNDS, 1)], far, far_sem, i, filed, 3, i)

    def late_near_copy(i, filed):
        return gather_copy(late_powers, late, late_sem, i, filed, 0, i)

    def late_far_copy(i, filed):
        return gather_copy(late_powers, late, late_sem, i, 32 + filed, 3, i)

    def turned_copy(i, filed):
        return gather_copy(turned_powers, late, late_sem, 32 + i, 64 + filed, 1, i)

    def each(count, action):
        def step(i, carry):
            action(i)
            return carry

        lax.fori_loop(0, count, step, 0)

    def raw_copy(j):
        return pltpu.make_async_copy(
            spectra_ref.at[:, pl.ds(pl.multiple_of(j * TILE, TILE), TILE), :], raw.at[j], raw_sem.at[j]
        )

    phase_copy = pltpu.make_async_copy(phases_ref.at[zl], phase, phase_sem.at[0])
    for j in range(QUAD):
        raw_copy(j).start()
    phase_copy.start()

    count = count_ref[0]
    lives = [jnp.where(w < count, 1.0, 0.0).astype(jnp.float32) for w in range(2)]

    def whiten(j, ahead=False):
        raw_copy(j).wait()

        def some_rows(r):
            rows = pl.ds(pl.multiple_of(r * 16, 16), 16)
            for w in range(2):
                mine = raw[j, w, rows, pl.ds(pl.multiple_of(zl * PART, PART), PART)].astype(jnp.float32)
                theirs = raw[j, w, rows, pl.ds(pl.multiple_of(second * PART, PART), PART)].astype(jnp.float32)
                square = jnp.sum(mine * mine + theirs * theirs, axis=1, keepdims=True)
                scaling = lax.rsqrt(square * (1.0 / (2 * PART)) + 1e-05) * lives[w]
                mine = (mine * scaling).astype(jnp.bfloat16)
                data[2 * zl, j, rows, w * PART : (w + 1) * PART] = mine
                data[2 * zl + 1, j, rows, w * PART : w * PART + FB] = mine[:, FB:]
                data[2 * zl + 1, j, rows, w * PART + FB : (w + 1) * PART] = -mine[:, :FB]
                zs[j, rows, w * PART : (w + 1) * PART] = (theirs * scaling).astype(jnp.bfloat16)

        each(TILE // 16, some_rows)
        if ahead:
            pl.semaphore_wait(barrier, 7)
        z_copy(j).start()
        up_copy(zl, j).start()
        dn_copy(zl, j).start()

    whiten(0, ahead=True)
    each(QUAD - 1, lambda j: whiten(j + 1))

    def flip_to(target, slab, j):
        def some_rows(r):
            rows = pl.ds(pl.multiple_of(r * 16, 16), 16)
            for w in range(2):
                target[rows, w * PART : w * PART + FB] = data[slab, j, rows, w * PART + FB : (w + 1) * PART]
                target[rows, w * PART + FB : (w + 1) * PART] = -data[slab, j, rows, w * PART : w * PART + FB]

        each(TILE // 16, some_rows)

    def flip(slab, j):
        flip_to(data.at[slab + 1, j], slab, j)

    phase_copy.wait()
    angles = phase[...]
    norm_factor = 1.0 / math.sqrt(TILE)
    cosine = (jnp.cos(angles) * norm_factor).astype(jnp.bfloat16)
    sine_part = (jnp.sin(angles) * norm_factor).astype(jnp.bfloat16)
    velocities = angles.shape[1]
    matrix[:TILE, :velocities] = cosine
    matrix[:TILE, velocities:] = sine_part
    matrix[TILE:, :velocities] = -sine_part
    matrix[TILE:, velocities:] = cosine
    total_weight = jnp.full((1, 2 * TILE), count, jnp.int32).astype(jnp.float32)
    total_weight = total_weight * math.sqrt(FB * lax.axis_size("seg"))

    def job(n, h):
        @pl.when(n == 1)
        def _():
            for jj in range(2):
                j = 2 * h + jj
                z_wait(j)
                up_copy(second, j).start()
                dn_copy(second, j).start()
                flip(2 * second, j)
                up_copy(first, j).wait_recv()
                dn_copy(first, j).wait_recv()
                flip(4 + 2 * first, j)

        left_slab = pick(n, [first, first, second, 0, second, 2 + first])
        right_slab = pick(n, [2 * first, 8 + first, 2 * second, 2, 8 + first, 8 + first])
        left_side = data[pl.ds(2 * left_slab, 2)].reshape(2 * QUAD * TILE, 2 * PART)
        right_side = data[right_slab, pl.ds(2 * h, 2)].reshape(2 * TILE, 2 * PART)
        product = multiply(left_side, right_side)
        product = (product / total_weight).astype(jnp.bfloat16).reshape(2, QUAD, TILE, 2 * TILE)
        for jj in range(2):
            columns = slice(jj * TILE, (jj + 1) * TILE)
            out[n, 2 * h + jj, :, :, :TILE] = product[0, :, :, columns]
            out[n, 2 * h + jj, :, :, TILE:] = product[1, :, :, columns]

    def multiply(left_side, right_side):
        return lax.dot_general(
            left_side, right_side, (((1,), (1,)), ((), ())), preferred_element_type=jnp.float32
        )

    def small_job(n, q, r, left_slab, left_chunk, right_slab, right_chunk):
        left_side = data[pl.ds(left_slab, 2), left_chunk].reshape(2 * TILE, 2 * PART)
        product = multiply(left_side, data[right_slab, right_chunk])
        product = (product / total_weight[:, :TILE]).astype(jnp.bfloat16)
        out[n, q, r, :, :TILE] = product[:TILE]
        out[n, q, r, :, TILE:] = product[TILE:]

    def chunk_job(n, j):
        up_copy(second, j).wait_recv()
        flip_to(column, 8 + second, j)
        left_side = jnp.concatenate([data[2 * first], data[2 * second]], axis=0)
        right_side = jnp.concatenate([data[8 + second, j], column[...]], axis=0)
        product = multiply(left_side.reshape(2 * QUAD * TILE, 2 * PART), right_side)
        product = (product / total_weight).reshape(2, QUAD, TILE, 2 * TILE)
        out[n, 0:2, :, :, :TILE] = product[:, :, :, :TILE].astype(jnp.bfloat16)
        out[n, 0:2, :, :, TILE:] = (-product[:, :, :, TILE:]).astype(jnp.bfloat16)
        dn_copy(second, j).wait_recv()
        flip(4 + 2 * second, j)

        def mixed(r):
            small_job(n, 2, r, 6, (1 - zl) * j + zl * r, 8, zl * j + (1 - zl) * r)

        each(QUAD, mixed)
        each(j + 1, lambda r: small_job(n, 3, r, 4 + 2 * second, r, 8 + second, j))

    def add_cores(n):
        core_copy(n).wait_recv()

        def one(t):
            q, r = t // 4, t % 4
            total = out[n, 2 * core + q, r].astype(jnp.float32) + core_in[n, q, r].astype(jnp.float32)
            out[n, 2 * core + q, r] = total.astype(jnp.bfloat16)

        each(8, one)
        for side in range(2):
            relay_copy(n, side).start()

    def add_relayed(n):
        for side in range(2):
            to = right if side else left
            relay_copy(n, side).wait_recv()
            total = out[n, 2 * core + side, to].astype(jnp.float32) + relay_in[n, side].astype(jnp.float32)
            out[n, 2 * core + side, to] = total.astype(jnp.bfloat16)
        for side in range(2):
            ring_copy(n, side).start()

    def add_ring(n):
        for side in range(2):
            ring_copy(n, side).wait_recv()

        def total(z):
            return (
                out[n, 2 * core + z, x].astype(jnp.float32)
                + ring_in[n, 0, z].astype(jnp.float32)
                + ring_in[n, 1, z].astype(jnp.float32)
            )

        zhi_out[n] = total(1 - zh).astype(jnp.bfloat16)
        zhi_copy(n).start()
        keep[n] = total(zh)

    def add_last(n):
        zhi_copy(n).wait_recv()
        stacked = (keep[n] + zhi_in[n].astype(jnp.float32)).astype(jnp.bfloat16)

        def power_of(field):
            squared = field * field
            energy = squared[:, :velocities] + squared[:, velocities:]
            return jnp.sum(energy, axis=0, keepdims=True) * (1.0 / TILE)

        power = power_of(jnp.dot(stacked, matrix[...], preferred_element_type=jnp.float32))
        if isinstance(n, int) and n >= WHOLE_ROUNDS:
            late_powers[n - WHOLE_ROUNDS] = power
            turn = (((0,), (0,)), ((), ()))
            real = lax.dot_general(stacked[:, :TILE], matrix[:TILE], turn, preferred_element_type=jnp.float32)
            imag = lax.dot_general(stacked[:, TILE:], matrix[TILE:], turn, preferred_element_type=jnp.float32)
            turned_powers[n - WHOLE_ROUNDS] = power_of(real - imag)
        else:
            powers[n] = power

    stages = (add_cores, add_relayed, add_ring, add_last)

    def step(n):
        each(2, lambda h: job(n, h))
        core_copy(n).start()
        for behind, stage in enumerate(stages):
            @pl.when(n >= 1 + behind)
            def _():
                stage(n - 1 - behind)

    each(WHOLE_ROUNDS, step)
    pl.semaphore_signal(token, inc=1, device_id=z_mate, device_id_type=MESH)
    steps = [*range(WHOLE_ROUNDS), 6, None, 7, None, 8, None, 9, None, None, None, None]
    for at in range(WHOLE_ROUNDS, len(steps)):
        n = steps[at]
        if n is not None:
            chunk_job(n, n - WHOLE_ROUNDS)
            core_copy(n).start()
        for behind, stage in enumerate(stages):
            before = steps[at - 1 - behind]
            if before is not None:
                stage(before)
        if at == WHOLE_ROUNDS + 1:
            pl.semaphore_wait(token, 1)
            pl.semaphore_signal(token_up, inc=1, device_id=y_up, device_id_type=MESH)
            pl.semaphore_signal(token_dn, inc=1, device_id=y_down, device_id_type=MESH)
        if at == WHOLE_ROUNDS + 3:
            pl.semaphore_wait(token_up, 1)
            pl.semaphore_wait(token_dn, 1)
            near[0] = powers[pl.ds(0, NEAR_ROUNDS)]
            each(31, lambda i: near_copy(i + 1, back(i + 1)).start())
            each(32, lambda i: far_copy(i, back(i)).start())

    late[0] = late_powers[...]
    corner = (core == 1) & (zh == 1)

    @pl.when(core == 0)
    def _():
        each(31, lambda i: late_near_copy(i + 1, back(i + 1)).start())

    @pl.when(core == 1)
    def _():
        each(32, lambda i: late_far_copy(i, back(i)).start())

    @pl.when(corner)
    def _():
        each(32, lambda i: turned_copy(i, back(i)).start())

    each(31, lambda i: near_copy(0, i + 1).wait_recv())
    each(32, lambda i: far_copy(0, i).wait_recv())

    def late_near_wait(k):
        offset = (k // 8) * 16 + core + 2 * (k % 8)

        @pl.when(offset > 0)
        def _():
            late_near_copy(0, offset).wait_recv()

    each(16, late_near_wait)
    each(16, lambda k: late_far_copy(0, (k // 8) * 16 + (1 - core) + 2 * (k % 8)).wait_recv())
    each(8, lambda k: turned_copy(0, (k // 4) * 16 + (3 - seg % 4) + 4 * (k % 4)).wait_recv())

    for c in range(CAP):
        for g in range(BANDS):
            kind, slot, place = [place_of[3 * (c * BANDS + g) + part] for part in range(3)]
            inside = jnp.where(kind == 2, 0, slot)
            row = jnp.where(kind == 0, near[inside, jnp.minimum(place, NEAR_ROUNDS - 1)], far[inside, 0])
            row = jnp.where(kind == 2, late[slot, jnp.minimum(place, QUAD - 1)], row)
            out_ref[0, 0, c, g : g + 1, :] = jnp.where(place_of[3 * CAP * BANDS] > c, row, jnp.zeros_like(row))

    def drain_exchange(j):
        z_copy(j).wait_send()
        for p in range(2):
            up_copy(p, j).wait_send()
            dn_copy(p, j).wait_send()

    each(QUAD, drain_exchange)

    def drain_rounds(n):
        core_copy(n).wait_send()
        for side in range(2):
            relay_copy(n, side).wait_send()
            ring_copy(n, side).wait_send()
        zhi_copy(n).wait_send()

    each(ROUNDS, drain_rounds)
    each(31, lambda i: near_copy(i + 1, 0).wait_send())
    each(32, lambda i: far_copy(i, 0).wait_send())

    @pl.when(core == 0)
    def _():
        each(31, lambda i: late_near_copy(i + 1, 0).wait_send())

    @pl.when(core == 1)
    def _():
        each(32, lambda i: late_far_copy(i, 0).wait_send())

    @pl.when(corner)
    def _():
        each(32, lambda i: turned_copy(i, 0).wait_send())


def find_slots(owner_row, block, seg):
    order_ids = jnp.arange(owner_row.shape[0], dtype=jnp.int32)
    mine = owner_row == seg
    rank_of = jnp.sum(jnp.where(mine[None, :] & (order_ids[None, :] < order_ids[:, None]), 1, 0), axis=1)
    matches = mine[None, :] & (rank_of[None, :] == jnp.arange(CAP, dtype=jnp.int32)[:, None])
    tile = jnp.sum(jnp.where(matches, order_ids[None, :], 0), axis=1)[:, None]
    zl, g = block % 2, jnp.arange(BANDS, dtype=jnp.int32)[None, :]
    k, p, q = tile // 16, (tile // 4) % 4, tile % 4
    reach = zl + k
    apart = reach // 2
    row_first = jnp.where(zl == g, 1, 0)
    column_first = jnp.where(reach % 2 == g, 1, 0)
    firsts = row_first + column_first
    whole = jnp.where(firsts == 2, 0, jnp.where(firsts == 0, 2, 3))
    whole = jnp.where(apart == 1, jnp.where(firsts == 2, 1, 4), whole)
    is_whole = jnp.where(apart == 0, 1, jnp.where(apart == 1, column_first, jnp.where(firsts == 2, 1, 0)))
    turned = jnp.where((apart == 2) & (firsts == 0) & (p > q), 1, 0)
    mixed = jnp.where((apart == 2) & (firsts == 1), 1, 0)
    by_row = jnp.where(mixed == 1, 1 - g, turned)
    chunk = jnp.where(by_row == 1, p, q)
    at_x = jnp.where((1 - is_whole) * by_row == 1, q, p)
    at_zh = jnp.where(is_whole == 1, q % 2, jnp.where(apart == 1, 1 - row_first, 1 - mixed))
    at_core = jnp.where(is_whole == 1, q // 2, jnp.where(apart == 1, 0, 1))
    source = at_x * 4 + at_zh * 2 + at_core
    slot = ((zl + g) % 2) * 16 + (source - seg + 16) % 16
    plane = jnp.where(apart == 2, 1 + turned, 0)
    kind = jnp.where(is_whole == 1, jnp.where(apart == 2, 1, 0), 2)
    slot = jnp.where(is_whole == 1, slot, plane * 32 + slot)
    place = jnp.where(is_whole == 1, jnp.where(apart == 2, 0, whole), chunk)
    places = jnp.stack([jnp.broadcast_to(part, (CAP, BANDS)) for part in (kind, slot, place)], axis=2)
    return jnp.concatenate([places.reshape(-1), jnp.sum(jnp.where(mine, 1, 0))[None]]).astype(jnp.int32)


def body(spectra, window_count, tile_owner, phases):
    velocities = phases.shape[2]
    bf16, f32 = jnp.bfloat16, jnp.float32
    dma = pltpu.SemaphoreType.DMA
    return pl.pallas_call(
        kernel,
        out_shape=jax.ShapeDtypeStruct((1, 1, CAP, BANDS, velocities), f32),
        in_specs=[pl.BlockSpec(memory_space=pltpu.SMEM)] * 2 + [pl.BlockSpec(memory_space=pl.ANY)] * 2,
        out_specs=pl.BlockSpec(memory_space=pltpu.VMEM),
        scratch_shapes=[
            pltpu.VMEM((QUAD, 2, TILE, 2 * PART), bf16),
            pltpu.VMEM((QUAD, TILE, 2 * PART), bf16),
            pltpu.VMEM((10, QUAD, TILE, 2 * PART), bf16),
            pltpu.VMEM((ROUNDS, 4, QUAD, TILE, 2 * TILE), bf16),
            pltpu.VMEM((ROUNDS, 2, QUAD, TILE, 2 * TILE), bf16),
            pltpu.VMEM((ROUNDS, 2, TILE, 2 * TILE), bf16),
            pltpu.VMEM((ROUNDS, 2, 2, TILE, 2 * TILE), bf16),
            pltpu.VMEM((ROUNDS, TILE, 2 * TILE), bf16),
            pltpu.VMEM((ROUNDS, TILE, 2 * TILE), bf16),
            pltpu.VMEM((ROUNDS, TILE, 2 * TILE), f32),
            pltpu.VMEM((TILE, velocities), f32),
            pltpu.VMEM((2 * TILE, 2 * velocities), bf16),
            pltpu.VMEM((TILE, 2 * PART), bf16),
            pltpu.VMEM((WHOLE_ROUNDS, 1, velocities), f32),
            pltpu.VMEM((QUAD, 1, velocities), f32),
            pltpu.VMEM((QUAD, 1, velocities), f32),
            pltpu.VMEM((32, NEAR_ROUNDS, 1, velocities), f32),
            pltpu.VMEM((32, 1, 1, velocities), f32),
            pltpu.VMEM((96, QUAD, 1, velocities), f32),
            dma((QUAD,)),
            dma((1,)),
            dma((2, QUAD)),
            dma((2, 2, QUAD)),
            dma((2, 2, QUAD)),
            dma((2, ROUNDS)),
            dma((2, ROUNDS, 2)),
            dma((2, ROUNDS, 2)),
            dma((2, ROUNDS)),
            dma((2, 32)),
            dma((2, 32)),
            dma((2, 96)),
            pltpu.SemaphoreType.REGULAR,
            pltpu.SemaphoreType.REGULAR,
            pltpu.SemaphoreType.REGULAR,
        ],
        compiler_params=pltpu.CompilerParams(vmem_limit_bytes=60 * 1024 * 1024, has_side_effects=True, collective_id=0),
    )(find_slots(tile_owner[0], lax.axis_index("blk"), lax.axis_index("seg")), window_count, spectra[0], phases)


def solution(mesh):
    placed = (P("seg", None, "blk", None), P("seg"), P("blk", None), P())
    return jax.shard_map(
        body,
        mesh=mesh,
        in_specs=placed,
        out_specs=P("blk", "seg", None, None, None),
        check_vma=False,
    )
```

time: 156 us -> 146 us (0.936)
  Pallas kernels: 150 us -> 140 us
    pallas_call x1, Pallas kernels: 150 us -> 140 us  [body(): pl.pallas_call(kernel, out_shape=jax.ShapeDtypeStruct((1, 1, CAP, BANDS,...]
where the time goes in v2:
time: 146 us
  Pallas kernels  140 us (96%)
  other arithmetic  3.59 us (2%)
  local copies, waits for them, and re-layouts  1.51 us (1%)
    pallas_call x1, Pallas kernels, body(): pl.pallas_call(kernel, out_shape=jax.ShapeDtypeStruct((1, 1, CAP, BANDS,...  140 us

profile of v2, /device:TPU:1, one launch (start us, length us, event | category | flops | bytes accessed | tf_op | source)
XLA Modules:
  0.0 145.6 jit_solution(9373072923268801910)
XLA Ops:
  0.7 1.3 fusion.11
  1.9 0.7 compare_bitcast_fusion
  2.6 0.1 select_reduce_fusion
  2.7 0.1 select_reduce_fusion.1
  3.0 0.1 add_select_fusion
  3.1 0.1 copy.6
  3.2 0.1 reshape.1161
  3.3 1.2 pad_add_fusion.1.place_of
  4.5 139.8 %shard_map.46 = f32[1,1,8,2,256]{4,3,2,1,0:T(2,128)} custom-call(s32[49]{0:T(128)} %pad_add_fusion.1.place_of, s32[1]{0:T(128)S(6)} %copy.8.count_ref, bf16[2,512,2048]{2,1,0:T(8,128)(2,1)} %bitcast.4, f32[2,128,256]{2,1,0:T(8,128)} %phases_ref.1), custom_call_target="tpu_custom_call" | custom-call | tf_op jit(solution)/shard_map/pallas_call | solution.py:438
  144.3 1.3 copy.9
  (7 shorter events, 0.1 us)

commit v3 on v2

--- a/solution.py
+++ b/solution.py
@@ -14,6 +14,22 @@
 QUAD = 4
 ROUNDS = 10
 NEAR_ROUNDS, WHOLE_ROUNDS = 5, 6
+SCHEDULE = " ".join((
+    "p0 c0 r0 g0",
+    "l0 T p1 p2",
+    "c1 p3 c2 r1",
+    "p4 c3 r2 g1",
+    "p5 c4 r3 g2",
+    "l1 U p6 c5",
+    "r4 g3 l2 p7",
+    "c6 r5 g4 l3",
+    "c7 r6 g5 l4",
+    "p8 r7 g6 l5",
+    "c8 g7 l6 p9",
+    "r8 c9 E g8",
+    "r9 D l7 l8",
+    "g9 F l9",
+))
 PART = 2 * FB
 MESH = pl.DeviceIdType.MESH
 
@@ -28,7 +44,7 @@
 def kernel(
     place_of, count_ref, spectra_ref, phases_ref, out_ref,
     raw, zs, data, out, core_in, relay_in, ring_in, zhi_in, zhi_out, keep,
-    phase, matrix, column, powers, late_powers, turned_powers, near, far, late,
+    phase, matrix, powers, late_powers, turned_powers, near, far, late,
     raw_sem, phase_sem, z_sem, up_sem, dn_sem, core_sem, relay_sem, ring_sem, zhi_sem,
     near_sem, far_sem, late_sem, token, token_up, token_dn,
 ):
@@ -185,7 +201,7 @@
     matrix[TILE:, :velocities] = -sine_part
     matrix[TILE:, velocities:] = cosine
     total_weight = jnp.full((1, 2 * TILE), count, jnp.int32).astype(jnp.float32)
-    total_weight = total_weight * math.sqrt(FB * lax.axis_size("seg"))
+    weight = 1.0 / (total_weight * math.sqrt(FB * lax.axis_size("seg")))
 
     def job(n, h):
         @pl.when(n == 1)
@@ -205,7 +221,7 @@
         left_side = data[pl.ds(2 * left_slab, 2)].reshape(2 * QUAD * TILE, 2 * PART)
         right_side = data[right_slab, pl.ds(2 * h, 2)].reshape(2 * TILE, 2 * PART)
         product = multiply(left_side, right_side)
-        product = (product / total_weight).astype(jnp.bfloat16).reshape(2, QUAD, TILE, 2 * TILE)
+        product = (product * weight).astype(jnp.bfloat16).reshape(2, QUAD, TILE, 2 * TILE)
         for jj in range(2):
             columns = slice(jj * TILE, (jj + 1) * TILE)
             out[n, 2 * h + jj, :, :, :TILE] = product[0, :, :, columns]
@@ -216,38 +232,31 @@
             left_side, right_side, (((1,), (1,)), ((), ())), preferred_element_type=jnp.float32
         )
 
-    def small_job(n, q, r, left_slab, left_chunk, right_slab, right_chunk):
-        left_side = data[pl.ds(left_slab, 2), left_chunk].reshape(2 * TILE, 2 * PART)
-        product = multiply(left_side, data[right_slab, right_chunk])
-        product = (product / total_weight[:, :TILE]).astype(jnp.bfloat16)
-        out[n, q, r, :, :TILE] = product[:TILE]
-        out[n, q, r, :, TILE:] = product[TILE:]
+    def store(n, q, left_side, right_side):
+        count_rows = left_side.shape[0]
+        product = multiply(left_side.reshape(count_rows * TILE, 2 * PART), right_side) * weight
+        product = product.reshape(count_rows, TILE, 2 * TILE)
+        for r in range(0, count_rows, QUAD):
+            rows = slice(r, min(r + QUAD, count_rows))
+            out[n, q + r // QUAD, : rows.stop - r, :, :TILE] = product[rows, :, :TILE].astype(jnp.bfloat16)
+            out[n, q + r // QUAD, : rows.stop - r, :, TILE:] = (-product[rows, :, TILE:]).astype(jnp.bfloat16)
 
     def chunk_job(n, j):
         up_copy(second, j).wait_recv()
-        flip_to(column, 8 + second, j)
-        left_side = jnp.concatenate([data[2 * first], data[2 * second]], axis=0)
-        right_side = jnp.concatenate([data[8 + second, j], column[...]], axis=0)
-        product = multiply(left_side.reshape(2 * QUAD * TILE, 2 * PART), right_side)
-        product = (product / total_weight).reshape(2, QUAD, TILE, 2 * TILE)
-        out[n, 0:2, :, :, :TILE] = product[:, :, :, :TILE].astype(jnp.bfloat16)
-        out[n, 0:2, :, :, TILE:] = (-product[:, :, :, TILE:]).astype(jnp.bfloat16)
+        flip_to(data.at[10, j], 8 + second, j)
+        chunk = jnp.concatenate([data[8 + second, j], data[10, j]], axis=0)
+        store(n, 0, jnp.concatenate([data[2 * first], data[2 * second]], axis=0), chunk)
         dn_copy(second, j).wait_recv()
         flip(4 + 2 * second, j)
-
-        def mixed(r):
-            small_job(n, 2, r, 6, (1 - zl) * j + zl * r, 8, zl * j + (1 - zl) * r)
-
-        each(QUAD, mixed)
-        each(j + 1, lambda r: small_job(n, 3, r, 4 + 2 * second, r, 8 + second, j))
+        store(n, 3, data[4 + 2 * second, 0 : j + 1], chunk)
+        store(n, 2, data[8 - 2 * zl], jnp.concatenate([data[6 + 2 * zl, j], data[7 + 3 * zl, j]], axis=0))
 
     def add_cores(n):
         core_copy(n).wait_recv()
 
         def one(t):
             q, r = t // 4, t % 4
-            total = out[n, 2 * core + q, r].astype(jnp.float32) + core_in[n, q, r].astype(jnp.float32)
-            out[n, 2 * core + q, r] = total.astype(jnp.bfloat16)
+            out[n, 2 * core + q, r] = out[n, 2 * core + q, r] + core_in[n, q, r]
 
         each(8, one)
         for side in range(2):
@@ -257,8 +266,7 @@
         for side in range(2):
             to = right if side else left
             relay_copy(n, side).wait_recv()
-            total = out[n, 2 * core + side, to].astype(jnp.float32) + relay_in[n, side].astype(jnp.float32)
-            out[n, 2 * core + side, to] = total.astype(jnp.bfloat16)
+            out[n, 2 * core + side, to] = out[n, 2 * core + side, to] + relay_in[n, side]
         for side in range(2):
             ring_copy(n, side).start()
 
@@ -287,84 +295,16 @@
             return jnp.sum(energy, axis=0, keepdims=True) * (1.0 / TILE)
 
         power = power_of(jnp.dot(stacked, matrix[...], preferred_element_type=jnp.float32))
-        if isinstance(n, int) and n >= WHOLE_ROUNDS:
-            late_powers[n - WHOLE_ROUNDS] = power
+        if n >= WHOLE_ROUNDS:
             turn = (((0,), (0,)), ((), ()))
             real = lax.dot_general(stacked[:, :TILE], matrix[:TILE], turn, preferred_element_type=jnp.float32)
             imag = lax.dot_general(stacked[:, TILE:], matrix[TILE:], turn, preferred_element_type=jnp.float32)
-            turned_powers[n - WHOLE_ROUNDS] = power_of(real - imag)
+            turned = power_of(real - imag)
+            turned_powers[n - WHOLE_ROUNDS] = turned
+            mirrored = (zl == 0) & (core == 1) & (zh == 0)
+            late_powers[n - WHOLE_ROUNDS] = jnp.where(mirrored, turned, power)
         else:
             powers[n] = power
-
-    stages = (add_cores, add_relayed, add_ring, add_last)
-
-    def step(n):
-        each(2, lambda h: job(n, h))
-        core_copy(n).start()
-        for behind, stage in enumerate(stages):
-            @pl.when(n >= 1 + behind)
-            def _():
-                stage(n - 1 - behind)
-
-    each(WHOLE_ROUNDS, step)
-    pl.semaphore_signal(token, inc=1, device_id=z_mate, device_id_type=MESH)
-    steps = [*range(WHOLE_ROUNDS), 6, None, 7, None, 8, None, 9, None, None, None, None]
-    for at in range(WHOLE_ROUNDS, len(steps)):
-        n = steps[at]
-        if n is not None:
-            chunk_job(n, n - WHOLE_ROUNDS)
-            core_copy(n).start()
-        for behind, stage in enumerate(stages):
-            before = steps[at - 1 - behind]
-            if before is not None:
-                stage(before)
-        if at == WHOLE_ROUNDS + 1:
-            pl.semaphore_wait(token, 1)
-            pl.semaphore_signal(token_up, inc=1, device_id=y_up, device_id_type=MESH)
-            pl.semaphore_signal(token_dn, inc=1, device_id=y_down, device_id_type=MESH)
-        if at == WHOLE_ROUNDS + 3:
-            pl.semaphore_wait(token_up, 1)
-            pl.semaphore_wait(token_dn, 1)
-            near[0] = powers[pl.ds(0, NEAR_ROUNDS)]
-            each(31, lambda i: near_copy(i + 1, back(i + 1)).start())
-            each(32, lambda i: far_copy(i, back(i)).start())
-
-    late[0] = late_powers[...]
-    corner = (core == 1) & (zh == 1)
-
-    @pl.when(core == 0)
-    def _():
-        each(31, lambda i: late_near_copy(i + 1, back(i + 1)).start())
-
-    @pl.when(core == 1)
-    def _():
-        each(32, lambda i: late_far_copy(i, back(i)).start())
-
-    @pl.when(corner)
-    def _():
-        each(32, lambda i: turned_copy(i, back(i)).start())
-
-    each(31, lambda i: near_copy(0, i + 1).wait_recv())
-    each(32, lambda i: far_copy(0, i).wait_recv())
-
-    def late_near_wait(k):
-        offset = (k // 8) * 16 + core + 2 * (k % 8)
-
-        @pl.when(offset > 0)
-        def _():
-            late_near_copy(0, offset).wait_recv()
-
-    each(16, late_near_wait)
-    each(16, lambda k: late_far_copy(0, (k // 8) * 16 + (1 - core) + 2 * (k % 8)).wait_recv())
-    each(8, lambda k: turned_copy(0, (k // 4) * 16 + (3 - seg % 4) + 4 * (k % 4)).wait_recv())
-
-    for c in range(CAP):
-        for g in range(BANDS):
-            kind, slot, place = [place_of[3 * (c * BANDS + g) + part] for part in range(3)]
-            inside = jnp.where(kind == 2, 0, slot)
-            row = jnp.where(kind == 0, near[inside, jnp.minimum(place, NEAR_ROUNDS - 1)], far[inside, 0])
-            row = jnp.where(kind == 2, late[slot, jnp.minimum(place, QUAD - 1)], row)
-            out_ref[0, 0, c, g : g + 1, :] = jnp.where(place_of[3 * CAP * BANDS] > c, row, jnp.zeros_like(row))
 
     def drain_exchange(j):
         z_copy(j).wait_send()
@@ -372,7 +312,6 @@
             up_copy(p, j).wait_send()
             dn_copy(p, j).wait_send()
 
-    each(QUAD, drain_exchange)
 
     def drain_rounds(n):
         core_copy(n).wait_send()
@@ -381,9 +320,81 @@
             ring_copy(n, side).wait_send()
         zhi_copy(n).wait_send()
 
-    each(ROUNDS, drain_rounds)
-    each(31, lambda i: near_copy(i + 1, 0).wait_send())
-    each(32, lambda i: far_copy(i, 0).wait_send())
+    def products(n):
+        if n < WHOLE_ROUNDS:
+            each(2, lambda h: job(n, h))
+        else:
+            chunk_job(n, n - WHOLE_ROUNDS)
+        core_copy(n).start()
+
+    def send_early():
+        pl.semaphore_wait(token_up, 1)
+        pl.semaphore_wait(token_dn, 1)
+        near[0] = powers[pl.ds(0, NEAR_ROUNDS)]
+        each(31, lambda i: near_copy(i + 1, back(i + 1)).start())
+        each(32, lambda i: far_copy(i, back(i)).start())
+
+    def drain_early():
+        each(31, lambda i: near_copy(0, i + 1).wait_recv())
+        each(32, lambda i: far_copy(0, i).wait_recv())
+        each(31, lambda i: near_copy(i + 1, 0).wait_send())
+        each(32, lambda i: far_copy(i, 0).wait_send())
+
+    def drain_first():
+        each(QUAD, drain_exchange)
+        each(ROUNDS - 2, drain_rounds)
+
+    def tell_pair():
+        pl.semaphore_signal(token, inc=1, device_id=z_mate, device_id_type=MESH)
+
+    def tell_planes():
+        pl.semaphore_wait(token, 1)
+        pl.semaphore_signal(token_up, inc=1, device_id=y_up, device_id_type=MESH)
+        pl.semaphore_signal(token_dn, inc=1, device_id=y_down, device_id_type=MESH)
+
+    acts = dict(p=products, c=add_cores, r=add_relayed, g=add_ring, l=add_last)
+    others = dict(T=tell_pair, U=tell_planes, E=send_early, D=drain_first, F=drain_early)
+    for event in SCHEDULE.split():
+        if event in others:
+            others[event]()
+        else:
+            acts[event[0]](int(event[1]))
+
+    late[0] = late_powers[...]
+    corner = (core == 1) & (zh == 1)
+
+    @pl.when(core == 0)
+    def _():
+        each(31, lambda i: late_near_copy(i + 1, back(i + 1)).start())
+
+    @pl.when(core == 1)
+    def _():
+        each(32, lambda i: late_far_copy(i, back(i)).start())
+
+    @pl.when(corner)
+    def _():
+        each(32, lambda i: turned_copy(i, back(i)).start())
+
+    def late_near_wait(k):
+        offset = (k // 8) * 16 + core + 2 * (k % 8)
+
+        @pl.when(offset > 0)
+        def _():
+            late_near_copy(0, offset).wait_recv()
+
+    each(16, late_near_wait)
+    each(16, lambda k: late_far_copy(0, (k // 8) * 16 + (1 - core) + 2 * (k % 8)).wait_recv())
+    each(8, lambda k: turned_copy(0, (k // 4) * 16 + (3 - seg % 4) + 4 * (k % 4)).wait_recv())
+
+    for c in range(CAP):
+        for g in range(BANDS):
+            kind, slot, place = [place_of[c, part * BANDS + g] for part in range(3)]
+            inside = jnp.where(kind < 2, slot, 0)
+            row = jnp.where(kind == 0, near[inside, jnp.minimum(place, NEAR_ROUNDS - 1)], far[inside, 0])
+            row = jnp.where(kind == 2, late[slot, jnp.minimum(place, QUAD - 1)], row)
+            out_ref[0, 0, c, g : g + 1, :] = jnp.where(kind < 3, row, jnp.zeros_like(row))
+
+    each(2, lambda n: drain_rounds(ROUNDS - 2 + n))
 
     @pl.when(core == 0)
     def _():
@@ -425,10 +436,11 @@
     slot = ((zl + g) % 2) * 16 + (source - seg + 16) % 16
     plane = jnp.where(apart == 2, 1 + turned, 0)
     kind = jnp.where(is_whole == 1, jnp.where(apart == 2, 1, 0), 2)
+    kind = jnp.where(jnp.sum(jnp.where(matches, 1, 0), axis=1)[:, None] == 1, kind, 3)
     slot = jnp.where(is_whole == 1, slot, plane * 32 + slot)
     place = jnp.where(is_whole == 1, jnp.where(apart == 2, 0, whole), chunk)
-    places = jnp.stack([jnp.broadcast_to(part, (CAP, BANDS)) for part in (kind, slot, place)], axis=2)
-    return jnp.concatenate([places.reshape(-1), jnp.sum(jnp.where(mine, 1, 0))[None]]).astype(jnp.int32)
+    parts = [jnp.broadcast_to(part, (CAP, BANDS)) for part in (kind, slot, place)]
+    return jnp.concatenate(parts, axis=1).astype(jnp.int32)
 
 
 def body(spectra, window_count, tile_owner, phases):
@@ -443,7 +455,7 @@
         scratch_shapes=[
             pltpu.VMEM((QUAD, 2, TILE, 2 * PART), bf16),
             pltpu.VMEM((QUAD, TILE, 2 * PART), bf16),
-            pltpu.VMEM((10, QUAD, TILE, 2 * PART), bf16),
+            pltpu.VMEM((11, QUAD, TILE, 2 * PART), bf16),
             pltpu.VMEM((ROUNDS, 4, QUAD, TILE, 2 * TILE), bf16),
             pltpu.VMEM((ROUNDS, 2, QUAD, TILE, 2 * TILE), bf16),
             pltpu.VMEM((ROUNDS, 2, TILE, 2 * TILE), bf16),
@@ -453,7 +465,6 @@
             pltpu.VMEM((ROUNDS, TILE, 2 * TILE), f32),
             pltpu.VMEM((TILE, velocities), f32),
             pltpu.VMEM((2 * TILE, 2 * velocities), bf16),
-            pltpu.VMEM((TILE, 2 * PART), bf16),
             pltpu.VMEM((WHOLE_ROUNDS, 1, velocities), f32),
             pltpu.VMEM((QUAD, 1, velocities), f32),
             pltpu.VMEM((QUAD, 1, velocities), f32),

time: 146 us -> 139 us (0.952)
  Pallas kernels: 140 us -> 135 us
  other arithmetic: 3.59 us -> 1.78 us
    pallas_call x1, Pallas kernels: 140 us -> 135 us  [body(): pl.pallas_call(kernel, out_shape=jax.ShapeDtypeStruct((1, 1, CAP, BANDS,...]
where the time goes in v3:
time: 139 us; the launch traced here: 138 us
  Pallas kernels  135 us (97%)
  other arithmetic  1.78 us (1%)
    pallas_call x1, Pallas kernels, body(): pl.pallas_call(kernel, out_shape=jax.ShapeDtypeStruct((1, 1, CAP, BANDS,...  135 us

profile of v3, /device:TPU:1, one launch (start us, length us, event | category | flops | bytes accessed | tf_op | source)
XLA Modules:
  0.0 138.4 jit_solution(15549930615546664656)
XLA Ops:
  0.7 0.7 compare_bitcast_fusion
  1.3 0.1 select_reduce_fusion
  1.4 0.2 select_reduce_fusion.2
  1.7 0.1 add_select_fusion
  1.8 0.7 pad_add_fusion.place_of
  2.5 134.6 %shard_map.46 = f32[1,1,8,2,256]{4,3,2,1,0:T(2,128)} custom-call(s32[8,6]{1,0:T(8,128)} %pad_add_fusion.place_of, s32[1]{0:T(128)S(6)} %copy.6.count_ref, bf16[2,512,2048]{2,1,0:T(8,128)(2,1)} %bitcast.3, f32[2,128,256]{2,1,0:T(8,128)} %phases_ref.1), custom_call_target="tpu_custom_call" | custom-call | tf_op jit(solution)/shard_map/pallas_call | solution.py:450
  137.1 1.3 copy.7
  (7 shorter events, 0.1 us)

commit v4 on v3

--- a/solution.py
+++ b/solution.py
@@ -450,7 +450,7 @@
     return pl.pallas_call(
         kernel,
         out_shape=jax.ShapeDtypeStruct((1, 1, CAP, BANDS, velocities), f32),
-        in_specs=[pl.BlockSpec(memory_space=pltpu.SMEM)] * 2 + [pl.BlockSpec(memory_space=pl.ANY)] * 2,
+        in_specs=[pl.BlockSpec(memory_space=pltpu.VMEM), pl.BlockSpec(memory_space=pltpu.SMEM)] + [pl.BlockSpec(memory_space=pl.ANY)] * 2,
         out_specs=pl.BlockSpec(memory_space=pltpu.VMEM),
         scratch_shapes=[
             pltpu.VMEM((QUAD, 2, TILE, 2 * PART), bf16),

time: 139 us -> 139 us (level)
  no operation moved by 1% of the time
where the time goes in v4:
time: 139 us; the launch traced here: 138 us
  Pallas kernels  135 us (97%)
  other arithmetic  1.78 us (1%)
    pallas_call x1, Pallas kernels, body(): pl.pallas_call(kernel, out_shape=jax.ShapeDtypeStruct((1, 1, CAP, BANDS,...  135 us

profile of v4, /device:TPU:1, one launch (start us, length us, event | category | flops | bytes accessed | tf_op | source)
XLA Modules:
  0.0 138.3 jit_solution(2607700945103070718)
XLA Ops:
  0.7 0.7 compare_bitcast_fusion
  1.3 0.1 select_reduce_fusion
  1.4 0.2 select_reduce_fusion.2
  1.7 0.1 add_select_fusion
  1.8 0.7 pad_add_fusion.place_of
  2.5 134.5 %shard_map.46 = f32[1,1,8,2,256]{4,3,2,1,0:T(2,128)} custom-call(s32[8,6]{1,0:T(8,128)} %pad_add_fusion.place_of, s32[1]{0:T(128)S(6)} %copy.6.count_ref, bf16[2,512,2048]{2,1,0:T(8,128)(2,1)} %bitcast.3, f32[2,128,256]{2,1,0:T(8,128)} %phases_ref.1), custom_call_target="tpu_custom_call" | custom-call | tf_op jit(solution)/shard_map/pallas_call | solution.py:450
  137.0 1.3 copy.7
  (7 shorter events, 0.1 us)
